TPU v7x, 32 devices: a whole 2x2x4 slice. The times are simulated.
32 devices in a mesh: row: 8 (over z, core), col: 4 (over y, x).
Axes of the slice: x: 2, y: 2, z: 4, core: 2. Of those that a mesh axis runs over, the one named last changes fastest.
Arguments:
- tile_left: bfloat16 [8, 4, 2048, 128], P('row', 'col'), may hold values from -6 to 6
- tile_right: bfloat16 [8, 4, 2048, 128], P('row', 'col'), may hold values from -1 to 1
- tile_blocks: int32 [8, 4], P('row', 'col'), may hold values from 1 to 4
- panel_left: bfloat16 [2, 8, 2048, 128], P(None, 'row', 'col'), may hold values from -6 to 6
- panel_right: bfloat16 [2, 8, 2048, 128], P(None, 'row', 'col'), may hold values from -2 to 2
- swap_flag: int32 [8, 4], P('row', 'col'), may hold values from 0 to 1, as said below
Outputs:
- grown_left: bfloat16 [8, 4, 2048, 256], P('row', 'col')
- grown_right: bfloat16 [8, 4, 2048, 256], P('row', 'col')
Inputs may be any that keep to these rules, and one draw needn't show every extreme that they name: swap_flag[i, c] equals swap_flag[i, (c + 4 / 2) mod 4], so tiles change owner in pairs.
All inputs are finite; a program needn't handle non-finite values.
Results may differ from a plain program's by a relative error of at most 0.0057.
Values may be sent and summed in bfloat16 or wider, within the bound.
A program may use at most 64 MiB of HBM per device.

v0:
```python
import functools

import jax
import jax.numpy as jnp
from jax import lax
from jax.experimental import pallas as pl
from jax.experimental.pallas import tpu as pltpu
from jax.sharding import PartitionSpec as P

RBLK = 32
MESH = pl.DeviceIdType.MESH
BF16 = jnp.bfloat16
F32 = jnp.float32


def exchange(R, C, u, v, pleft, pright, meta, stack, pair, uph, upm, inh, inm,
             ubuf, vbuf, uown, vown, pr1, rowbuf, colbuf, prbuf, psend, precv, mbuf, work,
             s_swap, r_swap, s_row, r_row, s_fwd, s_col, r_col, s_st, s_pr, r_pr, s_part, r_part, s_meta, r_meta,
             s_loc):
    r, c = lax.axis_index("row"), lax.axis_index("col")
    half = C // 2
    mate = lax.rem(c + half, C)
    sib = r + 1 - 2 * lax.rem(r, 2)
    has_up, has_dn = r + 2 < R, r >= 2
    nb, rk = u.shape
    blk, rp = pleft.shape[1:]
    n = rk + rp

    def rcopy(src, dst, ss, rs, to):
        return pltpu.make_async_remote_copy(
            src_ref=src, dst_ref=dst, send_sem=ss, recv_sem=rs, device_id=to, device_id_type=MESH
        )

    load_u = pltpu.make_async_copy(u, uown, s_loc.at[3])
    load_v = pltpu.make_async_copy(v, vown, s_loc.at[4])
    load_r = pltpu.make_async_copy(pright.at[1], pr1, s_loc.at[5])
    load_l = pltpu.make_async_copy(pleft.at[1], rowbuf.at[c], s_loc.at[6])
    load_r.start()
    load_l.start()
    load_u.start()
    load_v.start()

    barrier = pltpu.get_barrier_semaphore()
    for d in range(C):
        @pl.when(d != c)
        def _():
            pl.semaphore_signal(barrier, inc=1, device_id=(r, d), device_id_type=MESH)
    pl.semaphore_signal(barrier, inc=1, device_id=(sib, c), device_id_type=MESH)

    @pl.when(has_up)
    def _():
        pl.semaphore_signal(barrier, inc=1, device_id=(r + 2, c), device_id_type=MESH)

    @pl.when(has_dn)
    def _():
        pl.semaphore_signal(barrier, inc=1, device_id=(r - 2, c), device_id_type=MESH)

    peers = C + jnp.where(has_up, 1, 0) + jnp.where(has_dn, 1, 0)
    pl.semaphore_wait(barrier, peers)

    ends = []

    def send(cond, copy):
        @pl.when(cond)
        def _():
            copy.start()
        ends.append((cond, copy))

    loc_pr = pltpu.make_async_copy(pright.at[0], prbuf.at[lax.min(r, C - 1)], s_loc.at[0])
    is_src_pr = r < C

    def relay_sends(s, src, slot, ss, rs):
        par = lax.rem(r, 2) == lax.rem(s, 2)
        send(par & (r >= s) & has_up, rcopy(src, slot, ss.at[0], rs, (r + 2, c)))
        send(par & (r <= s) & has_dn, rcopy(src, slot, ss.at[1], rs, (r - 2, c)))
        send(par, rcopy(src, slot, ss.at[2], rs, (sib, c)))

    for d in range(C):
        send(c != d, rcopy(meta, mbuf.at[c], s_meta.at[d], r_meta.at[c], (r, d)))

    for s in range(C):
        slot, rs, ss = prbuf.at[s], r_pr.at[s], s_pr.at[s]
        send((r == s) & has_up, rcopy(pright.at[0], slot, ss.at[0], rs, (r + 2, c)))
        send((r == s) & has_dn, rcopy(pright.at[0], slot, ss.at[1], rs, (r - 2, c)))
        send(r == s, rcopy(pright.at[0], slot, ss.at[2], rs, (sib, c)))

    @pl.when(is_src_pr)
    def _():
        loc_pr.start()

    for t in range(2):
        d = lax.rem(r + t * half, C)
        send((r < C) & (d != c), rcopy(pleft.at[0], colbuf.at[t, c], s_st.at[t], r_col.at[t, c], (r, d)))
    tiles = (c, mate)
    loc_pl = []
    for t in range(2):
        copy = pltpu.make_async_copy(pleft.at[0], colbuf.at[t, c], s_loc.at[1 + t])
        loc_pl.append(copy)

        @pl.when(r == tiles[t])
        def _():
            copy.start()

    for d in range(C):
        same = (c // half) == d // half
        send((c != d) & (same | (mate == d)),
             rcopy(pleft.at[1], rowbuf.at[c], s_row.at[d], r_row.at[c], (r, d)))
    swap_u = rcopy(u, ubuf, s_swap.at[0], r_swap.at[0], (r, mate))
    swap_v = rcopy(v, vbuf, s_swap.at[1], r_swap.at[1], (r, mate))

    for s in range(C):
        slot, rs, ss = prbuf.at[s], r_pr.at[s], s_pr.at[s]

        @pl.when(r != s)
        def _():
            rcopy(slot, slot, ss.at[0], rs, (sib, c)).wait_recv()

        par = lax.rem(r, 2) == s % 2
        send(par & (r > s) & has_up, rcopy(slot, slot, ss.at[0], rs, (r + 2, c)))
        send(par & (r < s) & has_dn, rcopy(slot, slot, ss.at[1], rs, (r - 2, c)))
        send(par & (r != s), rcopy(slot, slot, ss.at[2], rs, (sib, c)))

    rcopy(pleft.at[1], rowbuf.at[mate], s_row.at[0], r_row.at[mate], (r, mate)).wait_recv()
    for d in range(C):
        same = (c // half) == d // half
        send((c != d) & same, rcopy(rowbuf.at[mate], rowbuf.at[mate], s_fwd.at[d], r_row.at[mate], (r, d)))

    swap_u.start()

    @pl.when(is_src_pr)
    def _():
        loc_pr.wait()

    for d in range(C):
        @pl.when(c != d)
        def _():
            rcopy(meta, mbuf.at[d], s_meta.at[d], r_meta.at[d], (r, d)).wait_recv()

        @pl.when(c == d)
        def _():
            mbuf[d] = meta[...]

    load_r.wait()
    part = [
        lax.dot_general(pr1[...], prbuf[s], (((0,), (0,)), ((), ())), preferred_element_type=F32)
        for s in range(C)
    ]
    for d in range(C):
        chosen = mbuf[d][0:1, :] > 0.5
        value = jnp.where(chosen, part[(d + half) % C], part[d])
        psend[d] = value

        @pl.when(c == d)
        def _():
            precv[d] = value
    for d in range(C):
        send(c != d, rcopy(psend.at[d], precv.at[c], s_part.at[d], r_part.at[c], (r, d)))

    swap_v.start()

    for b in range(C):
        for t in range(2):
            slot, rs, ss = colbuf.at[t, b], r_col.at[t, b], s_col.at[t, b]
            mine = (r == tiles[t]) & (c == b)

            @pl.when(mine)
            def _():
                loc_pl[t].wait()

            @pl.when(jnp.logical_not(mine))
            def _():
                rcopy(slot, slot, ss.at[0], rs, (sib, c)).wait_recv()

            relay_sends(tiles[t], slot, slot, ss, rs)

    own_meta = meta[...]
    flagged = own_meta[0:1, :] > 0.5
    chosen_meta = jnp.where(flagged, mbuf[mate], own_meta)
    lane = lax.broadcasted_iota(jnp.int32, (1, rk), 1).astype(F32)
    live = lane < chosen_meta[1:2, :] * RBLK
    zero = jnp.zeros((), BF16)

    load_l.wait()
    for d in range(C):
        @pl.when((c != d) & (mate != d))
        def _():
            rcopy(pleft.at[1], rowbuf.at[d], s_row.at[d], r_row.at[d], (r, d)).wait_recv()
    load_u.wait()
    swap_u.wait_recv()
    for d in range(C):
        @pl.when(c != d)
        def _():
            rcopy(psend.at[d], precv.at[d], s_part.at[d], r_part.at[d], (r, d)).wait_recv()
    total = precv[0]
    for d in range(1, C):
        total = total + precv[d]
    coup = total.astype(BF16)

    def fill(step, acc):
        at = pl.ds(pl.multiple_of(step * blk, blk), blk)
        lifted = -jnp.dot(rowbuf[step], coup, preferred_element_type=F32)
        left = jnp.where(flagged, ubuf[at, :], uown[at, :])
        piece = jnp.concatenate([jnp.where(live, left, zero), lifted.astype(BF16)], axis=1)
        stack[at, :] = piece
        return acc + lax.dot_general(piece, piece, (((0,), (0,)), ((), ())), preferred_element_type=F32)

    gram = lax.fori_loop(0, C, fill, jnp.zeros((n, n), F32)) / nb
    ri = lax.broadcasted_iota(jnp.int32, (n, n), 0)
    ci = lax.broadcasted_iota(jnp.int32, (n, n), 1)
    dead = jnp.concatenate([jnp.where(live, 0.0, 1.0).astype(F32), jnp.zeros((1, rp), F32)], axis=1)
    work[:, :n] = gram + jnp.where(ri == ci, dead, 0.0)
    work[:, n:] = jnp.where(ri == ci, 1.0, 0.0).astype(F32)
    factor_rows(work, n, 32)
    upper = jnp.where(ri <= ci, work[:, :n], 0.0)
    inverse = work[:, n:]
    uph[...], upm[...], _ = split3(upper)
    inh[...], inm[...], _ = split3(inverse)

    load_v.wait()
    swap_v.wait_recv()

    def fill_right(step, _):
        at = pl.ds(pl.multiple_of(step * blk, blk), blk)
        right = jnp.where(flagged, vbuf[at, :], vown[at, :])
        own = jnp.where(flagged, colbuf[1, step], colbuf[0, step])
        pair[at, :] = jnp.concatenate([jnp.where(live, right, zero), own], axis=1)
        return 0

    lax.fori_loop(0, C, fill_right, 0)

    swap_u.wait_send()
    swap_v.wait_send()
    for cond, copy in ends:
        @pl.when(cond)
        def _():
            copy.wait_send()


def split3(x):
    h = x.astype(BF16)
    rest = x - h.astype(F32)
    m = rest.astype(BF16)
    return h, m, (rest - m.astype(F32)).astype(BF16)


def factor_rows(work, n, sb):
    lanes = 128
    sub = lax.broadcasted_iota(jnp.int32, (8, lanes), 0)
    groups = sb // 8

    def sub_row(x, k):
        return jnp.broadcast_to(x[k : k + 1, :], x.shape)

    for r0 in range(0, n, sb):
        a0 = r0 // lanes * lanes
        width = n + lanes
        tiles = width // lanes
        rows = [
            [work[r0 + 8 * g : r0 + 8 * g + 8, a0 + lanes * w : a0 + lanes * (w + 1)] for w in range(tiles)]
            for g in range(groups)
        ]
        for t in range(groups):
            base = r0 - a0 + 8 * t
            cols = [
                {g: jnp.broadcast_to(rows[g][0][:, base + i : base + i + 1], (8, lanes)) for g in range(t, groups)}
                for i in range(8)
            ]
            for k in range(8):
                inv = lax.rsqrt(sub_row(cols[k][t], k))
                scaled = {g: cols[k][g] * inv for g in range(t, groups)}
                for j in range(k + 1, 8):
                    lj = sub_row(scaled[t], j)
                    for g in range(t, groups):
                        cols[j][g] = cols[j][g] - scaled[g] * lj
                below = jnp.where(sub > k, scaled[t], 0.0)
                for w in range(tiles):
                    rowk = sub_row(rows[t][w], k) * inv
                    rows[t][w] = jnp.where(sub == k, rowk, rows[t][w] - below * rowk)
                    for g in range(t + 1, groups):
                        rows[g][w] = rows[g][w] - scaled[g] * rowk
        done = jnp.concatenate([jnp.concatenate(rows[g], axis=1) for g in range(groups)], axis=0)
        work[r0 : r0 + sb, a0 : a0 + width] = done
        r1 = r0 + sb
        if r1 < n:
            b0 = r1 // lanes * lanes
            h, m, l = split3(done)
            left = jnp.concatenate([h, h, m, m, h, l], axis=0)[:, b0 - a0 : n - a0]
            right = jnp.concatenate([h, m, h, m, l, h], axis=0)
            update = lax.dot_general(left, right, (((0,), (0,)), ((), ())), preferred_element_type=F32)
            work[r1:n, a0 : a0 + width] = work[r1:n, a0 : a0 + width] - update[r1 - b0 :, :]


def products(x, y, uph, upm, inh, inm, lo, ro):
    nt = (((1,), (1,)), ((), ()))

    def product(value, high, low):
        out = lax.dot_general(value, high[...], nt, preferred_element_type=F32)
        return (out + lax.dot_general(value, low[...], nt, preferred_element_type=F32)).astype(BF16)

    lo[...] = product(x[...], inh, inm)
    ro[...] = product(y[...], uph, upm)


def per_device(R, C, tile_left, tile_right, tile_blocks, panel_left, panel_right, swap_flag):
    nb, rk = tile_left.shape[2:]
    blk, rp = panel_left.shape[2:]
    n = rk + rp
    top = lax.broadcasted_iota(jnp.int32, (8, 128), 0) == 0
    meta = jnp.where(top, swap_flag[0, 0], tile_blocks[0, 0]).astype(F32)
    vm = pl.BlockSpec(memory_space=pltpu.VMEM)
    hbm = pl.BlockSpec(memory_space=pltpu.HBM)
    dma = pltpu.SemaphoreType.DMA
    S = jax.ShapeDtypeStruct
    V = pltpu.VMEM
    parts = pl.pallas_call(
        functools.partial(exchange, R, C),
        out_shape=(S((nb, n), BF16),) * 2 + (S((n, n), BF16),) * 4,
        in_specs=[hbm] * 4 + [vm],
        out_specs=[vm] * 6,
        scratch_shapes=[
            V((nb, rk), BF16), V((nb, rk), BF16), V((nb, rk), BF16), V((nb, rk), BF16), V((blk, rp), BF16),
            V((C, blk, rp), BF16), V((2, C, blk, rp), BF16), V((C, blk, rp), BF16),
            V((C, rp, rp), F32), V((C, rp, rp), F32), V((C, 8, 128), F32), V((n, 2 * n), F32),
            dma((2,)), dma((2,)), dma((C,)), dma((C,)), dma((C,)), dma((2, C, 3)), dma((2, C)), dma((2,)),
            dma((C, 3)), dma((C,)), dma((C,)), dma((C,)), dma((C,)), dma((C,)), dma((7,)),
        ],
        compiler_params=pltpu.CompilerParams(
            collective_id=0, has_side_effects=True, vmem_limit_bytes=58 * 1024 * 1024
        ),
        name="exchange",
    )(tile_left[0, 0], tile_right[0, 0], panel_left[:, 0], panel_right[:, 0], meta)
    piece = pl.BlockSpec((min(512, nb), n), lambda i: (i, 0))
    lo, ro = pl.pallas_call(
        products,
        grid=(nb // min(512, nb),),
        out_shape=(S((nb, n), BF16),) * 2,
        in_specs=[piece] * 2 + [pl.BlockSpec((n, n), lambda i: (0, 0))] * 4,
        out_specs=[piece] * 2,
        name="products",
    )(*parts)
    return lo[None, None], ro[None, None]


def solution(mesh):
    placed = (
        P("row", "col", None, None),
        P("row", "col", None, None),
        P("row", "col"),
        P(None, "row", "col", None),
        P(None, "row", "col", None),
        P("row", "col"),
    )
    return jax.shard_map(
        functools.partial(per_device, mesh.shape["row"], mesh.shape["col"]),
        mesh=mesh,
        in_specs=placed,
        out_specs=(P("row", "col", None, None), P("row", "col", None, None)),
        check_vma=False,
    )
```

profile of v0, /device:TPU:29, one launch (start us, length us, event | category | flops | bytes accessed | tf_op | source)
XLA Modules:
  0.0 69.9 jit_solution(17768471777900776890)
XLA Ops:
  1.9 0.7 iota.7.meta
  2.6 62.5 %exchange.1 = (bf16[2048,256]{1,0:T(8,128)(2,1)}, bf16[2048,256]{1,0:T(8,128)(2,1)}, bf16[256,256]{1,0:T(8,128)(2,1)}, bf16[256,256]{1,0:T(8,128)(2,1)}, bf16[25...) custom-call(bf16[2048,128]{1,0:T(8,128)(2,1)} %bitcast.10, bf16[2048,128]{1,0:T(8,128)(2,1)} %bitcast.11, ...), custom_call_target="tpu_custom_call" | custom-call | tf_op jit(solution)/shard_map/exchange/pallas_call | solution.py:315
  65.1 4.8 %products.1 = (bf16[2048,256]{1,0:T(8,128)(2,1)}, bf16[2048,256]{1,0:T(8,128)(2,1)}) custom-call(bf16[2048,256]{1,0:T(8,128)(2,1)} %get-tuple-element.10.x, bf16[2048,256]{1,0:T(8,128)(2,1)} %get-tuple-element.11.y, bf16[256,256]{1,0:T(8,128)(2,1)} %get-tuple-element.12.uph, bf16[256,256]{1,0:T(8,128)(2,1)} %get-tuple-element.13.upm, ...), custom_call_target="tpu_custom_call" | custom-call | tf_op jit(solution)/shard_map/products/pallas_call | solution.py:333
  (1 shorter events, 0.0 us)
where the time goes:
time: 70.1 us; the launch traced here: 69.9 us
  Pallas kernels  67.3 us (96%)
  between operations  1.94 us (3%)
    pallas_call x1, Pallas kernels, per_device(): pl.pallas_call(functools.partial(exchange, R, C), out_shape=(S((nb, n), B...  62.5 us
    pallas_call x1, Pallas kernels, per_device(): pl.pallas_call(products, grid=(nb // min(512, nb),), out_shape=(S((nb, n)...  4.8 us

commit v1 on v0

v1 whole, which is shorter than its diff:
```python
import functools

import jax
import jax.numpy as jnp
from jax import lax
from jax.experimental import pallas as pl
from jax.experimental.pallas import tpu as pltpu
from jax.sharding import PartitionSpec as P

RBLK = 32
MESH = pl.DeviceIdType.MESH
BF16 = jnp.bfloat16
F32 = jnp.float32
TN = (((0,), (0,)), ((), ()))
NT = (((1,), (1,)), ((), ()))


def update(R, C, NV, u, v, pleft, pright, blocks, swap, lo, ro,
           ubuf, vbuf, uown, vown, pr1, rowbuf, colbuf, prbuf, part, psend, precv, mine, mbuf, stack, work, sblk, sswp,
           s_u, r_u, s_v, r_v, s_row, r_row, s_fwd, s_col, r_col, s_st, s_pr, r_pr, s_part, r_part, s_meta, r_meta,
           s_loc):
    r, c = lax.axis_index("row"), lax.axis_index("col")
    half = C // 2
    mate = lax.rem(c + half, C)
    sib = r + 1 - 2 * lax.rem(r, 2)
    has_up, has_dn = r + 2 < R, r >= 2
    nb, rk = u.shape
    blk, rp = pleft.shape[1:]
    n = rk + rp
    tiles = (c, mate)

    def rcopy(src, dst, ss, rs, to):
        return pltpu.make_async_remote_copy(
            src_ref=src, dst_ref=dst, send_sem=ss, recv_sem=rs, device_id=to, device_id_type=MESH
        )

    load_b = pltpu.make_async_copy(blocks, sblk, s_loc.at[0])
    load_s = pltpu.make_async_copy(swap, sswp, s_loc.at[1])
    load_r = pltpu.make_async_copy(pright.at[1], pr1, s_loc.at[2])
    load_l = pltpu.make_async_copy(pleft.at[1], rowbuf.at[c], s_loc.at[3])
    load_u = pltpu.make_async_copy(u, uown, s_loc.at[4])
    load_v = pltpu.make_async_copy(v, vown, s_loc.at[5])
    load_p = pltpu.make_async_copy(pright.at[0], prbuf.at[lax.min(r, C - 1)], s_loc.at[6])
    load_c = [pltpu.make_async_copy(pleft.at[0], colbuf.at[t, c], s_loc.at[7 + t]) for t in range(2)]
    for copy in (load_b, load_s, load_r, load_l, load_u, load_v):
        copy.start()

    @pl.when(r < C)
    def _():
        load_p.start()

    for t in range(2):
        @pl.when(r == tiles[t])
        def _():
            load_c[t].start()

    barrier = pltpu.get_barrier_semaphore()
    for d in range(C):
        @pl.when(d != c)
        def _():
            pl.semaphore_signal(barrier, inc=1, device_id=(r, d), device_id_type=MESH)
    pl.semaphore_signal(barrier, inc=1, device_id=(sib, c), device_id_type=MESH)

    @pl.when(has_up)
    def _():
        pl.semaphore_signal(barrier, inc=1, device_id=(r + 2, c), device_id_type=MESH)

    @pl.when(has_dn)
    def _():
        pl.semaphore_signal(barrier, inc=1, device_id=(r - 2, c), device_id_type=MESH)

    load_b.wait()
    load_s.wait()
    top = lax.broadcasted_iota(jnp.int32, (8, 128), 0) == 0
    own_meta = jnp.where(top, sswp[0, 0], sblk[0, 0]).astype(F32)
    mine[...] = own_meta
    pl.semaphore_wait(barrier, C + jnp.where(has_up, 1, 0) + jnp.where(has_dn, 1, 0))

    ends = []

    def send(cond, copy):
        @pl.when(cond)
        def _():
            copy.start()
        ends.append((cond, copy))

    for d in range(C):
        send(c != d, rcopy(mine, mbuf.at[c], s_meta.at[d], r_meta.at[c], (r, d)))
    at_r = lax.min(r, C - 1)
    own_pr = (prbuf.at[at_r], s_pr.at[at_r], r_pr.at[at_r])
    for k, (cond, to) in enumerate(((has_up, r + 2), (has_dn, r - 2), (True, sib))):
        send((r < C) & cond, rcopy(pright.at[0], own_pr[0], own_pr[1].at[k], own_pr[2], (to, c)))
    for d in range(C):
        send((c != d) & (mate == d), rcopy(pleft.at[1], rowbuf.at[c], s_row.at[d], r_row.at[c], (r, d)))
    for d in range(C):
        same = (c // half) == d // half
        send((c != d) & same & (mate != d), rcopy(pleft.at[1], rowbuf.at[c], s_row.at[d], r_row.at[c], (r, d)))
    for t in range(2):
        d = lax.rem(r + t * half, C)
        send((r < C) & (d != c), rcopy(pleft.at[0], colbuf.at[t, c], s_st.at[t], r_col.at[t, c], (r, d)))

    for t in range(2):
        slot, rs, ss = colbuf.at[t, c], r_col.at[t, c], s_col.at[t, c]
        for k, (cond, to) in enumerate(((has_up, r + 2), (has_dn, r - 2), (True, sib))):
            send((r == tiles[t]) & cond, rcopy(pleft.at[0], slot, ss.at[k], rs, (to, c)))
    swap_u = rcopy(u, ubuf, s_u, r_u, (r, mate))
    swap_u.start()

    load_r.wait()

    @pl.when(r < C)
    def _():
        load_p.wait()

    def forward_row():
        rcopy(pleft.at[1], rowbuf.at[mate], s_row.at[0], r_row.at[mate], (r, mate)).wait_recv()
        for d in range(C):
            same = (c // half) == d // half
            send((c != d) & same, rcopy(rowbuf.at[mate], rowbuf.at[mate], s_fwd.at[d], r_row.at[mate], (r, d)))

    pairs = C // 2
    near = [2 * jnp.where(r // 2 + k < pairs, r // 2 + k, pairs - 1 - k) for k in range(pairs)]
    for w in range(2):
        for k in range(pairs):
            s = near[k] + lax.rem(r + w, 2)
            slot, rs, ss = prbuf.at[s], r_pr.at[s], s_pr.at[s]

            @pl.when(r != s)
            def _():
                rcopy(slot, slot, ss.at[0], rs, (sib, c)).wait_recv()

            if w == 0:
                send((r > s) & has_up, rcopy(slot, slot, ss.at[0], rs, (r + 2, c)))
                send((r < s) & has_dn, rcopy(slot, slot, ss.at[1], rs, (r - 2, c)))
                send(r != s, rcopy(slot, slot, ss.at[2], rs, (sib, c)))
            part[s] = lax.dot_general(pr1[...], prbuf[s], TN, preferred_element_type=F32)
        if w == 0:
            forward_row()

    for d in range(C):
        @pl.when(c != d)
        def _():
            rcopy(mine, mbuf.at[d], s_meta.at[d], r_meta.at[d], (r, d)).wait_recv()

        @pl.when(c == d)
        def _():
            mbuf[d] = own_meta

    flagged = own_meta[0:1, :] > 0.5
    for d in range(C):
        psend[d] = jnp.where(mbuf[d][0:1, :] > 0.5, part[(d + half) % C], part[d]).astype(BF16)
    total = jnp.where(flagged, part[mate], part[c])
    for d in range(C):
        send((c != d) & (mate == d), rcopy(psend.at[d], precv.at[c], s_part.at[d], r_part.at[c], (r, d)))
    for d in range(C):
        send((c != d) & (mate != d), rcopy(psend.at[d], precv.at[c], s_part.at[d], r_part.at[c], (r, d)))

    vb = nb // NV
    swap_v = [rcopy(v.at[pl.ds(k * vb, vb)], vbuf.at[pl.ds(k * vb, vb)], s_v.at[k], r_v.at[k], (r, mate))
              for k in range(NV)]
    for copy in swap_v:
        copy.start()

    def away(t):
        return jnp.abs(r // 2 - tiles[t] // 2)

    first = jnp.where(away(1) < away(0), 1, 0)
    for t in (first, 1 - first):
        home = jnp.where(t == 0, c, mate)
        par = lax.rem(r, 2) == lax.rem(home, 2)
        for k in range(C):
            b = lax.rem(c + k, half) + half * lax.rem(c // half + k // half, 2)
            slot, rs, ss = colbuf.at[t, b], r_col.at[t, b], s_col.at[t, b]
            relay = par & ((r != home) | (c != b))

            @pl.when(relay)
            def _():
                rcopy(slot, slot, ss.at[0], rs, (sib, c)).wait_recv()

            send(relay & (r >= home) & has_up, rcopy(slot, slot, ss.at[0], rs, (r + 2, c)))
            send(relay & (r <= home) & has_dn, rcopy(slot, slot, ss.at[1], rs, (r - 2, c)))
            send(relay, rcopy(slot, slot, ss.at[2], rs, (sib, c)))

    chosen_meta = jnp.where(flagged, mbuf[mate], own_meta)
    lane = lax.broadcasted_iota(jnp.int32, (1, rk), 1).astype(F32)
    live = lane < chosen_meta[1:2, :] * RBLK
    zero = jnp.zeros((), BF16)

    load_l.wait()
    for d in range(C):
        @pl.when((c != d) & (mate != d))
        def _():
            rcopy(pleft.at[1], rowbuf.at[d], s_row.at[d], r_row.at[d], (r, d)).wait_recv()
    load_u.wait()
    swap_u.wait_recv()
    for d in range(C):
        @pl.when(c != d)
        def _():
            rcopy(psend.at[d], precv.at[d], s_part.at[d], r_part.at[d], (r, d)).wait_recv()

        @pl.when(c == d)
        def _():
            precv[d] = jnp.zeros((rp, rp), BF16)
    for d in range(C):
        total = total + precv[d].astype(F32)
    coup = total.astype(BF16)

    def fill(step, acc):
        at = pl.ds(pl.multiple_of(step * blk, blk), blk)
        lifted = -jnp.dot(rowbuf[step], coup, preferred_element_type=F32)
        left = jnp.where(flagged, ubuf[at, :], uown[at, :])
        piece = jnp.concatenate([jnp.where(live, left, zero), lifted.astype(BF16)], axis=1)
        stack[at, :] = piece
        return acc + lax.dot_general(piece, piece, TN, preferred_element_type=F32)

    gram = lax.fori_loop(0, C, fill, jnp.zeros((n, n), F32)) / nb
    ri = lax.broadcasted_iota(jnp.int32, (n, n), 0)
    ci = lax.broadcasted_iota(jnp.int32, (n, n), 1)
    dead = jnp.concatenate([jnp.where(live, 0.0, 1.0).astype(F32), jnp.zeros((1, rp), F32)], axis=1)
    work[:, :n] = gram + jnp.where(ri == ci, dead, 0.0)
    work[:, n:] = jnp.where(ri == ci, 1.0, 0.0).astype(F32)
    factor_rows(work, n, 32)
    uph, upm, _ = split3(jnp.where(ri <= ci, work[:, :n], 0.0))
    inh, inm, _ = split3(work[:, n:])

    def product(value, high, low):
        out = lax.dot_general(value, high, NT, preferred_element_type=F32)
        return (out + lax.dot_general(value, low, NT, preferred_element_type=F32)).astype(BF16)

    def left_step(step, _):
        at = pl.ds(pl.multiple_of(step * vb, vb), vb)
        lo[at, :] = product(stack[at, :], inh, inm)
        return 0

    lax.fori_loop(0, NV, left_step, 0)

    load_v.wait()
    for t in range(2):
        @pl.when(r == tiles[t])
        def _():
            load_c[t].wait()

        for b in range(C):
            @pl.when(lax.rem(r, 2) != lax.rem(tiles[t], 2))
            def _():
                rcopy(colbuf.at[t, b], colbuf.at[t, b], s_col.at[t, b, 0], r_col.at[t, b], (sib, c)).wait_recv()

    for k in range(NV):
        swap_v[k].wait_recv()
        at = pl.ds(k * vb, vb)
        right = jnp.where(live, jnp.where(flagged, vbuf[at, :], vown[at, :]), zero)
        first, count = k * vb // blk, max(vb // blk, 1)
        cols = pl.ds(k * vb % blk, min(vb, blk))
        own = [jnp.where(flagged, colbuf[1, first + i, cols, :], colbuf[0, first + i, cols, :]) for i in range(count)]
        pair = jnp.concatenate([right, jnp.concatenate(own, axis=0)], axis=1)
        ro[at, :] = product(pair, uph, upm)

    swap_u.wait_send()
    for copy in swap_v:
        copy.wait_send()
    for cond, copy in ends:
        @pl.when(cond)
        def _():
            copy.wait_send()


def split3(x):
    h = x.astype(BF16)
    rest = x - h.astype(F32)
    m = rest.astype(BF16)
    return h, m, (rest - m.astype(F32)).astype(BF16)


def factor_rows(work, n, sb):
    lanes = 128
    sub = lax.broadcasted_iota(jnp.int32, (8, lanes), 0)
    groups = sb // 8

    def sub_row(x, k):
        return jnp.broadcast_to(x[k : k + 1, :], x.shape)

    for r0 in range(0, n, sb):
        a0 = r0 // lanes * lanes
        width = n + lanes
        tiles = width // lanes
        rows = [
            [work[r0 + 8 * g : r0 + 8 * g + 8, a0 + lanes * w : a0 + lanes * (w + 1)] for w in range(tiles)]
            for g in range(groups)
        ]
        for t in range(groups):
            base = r0 - a0 + 8 * t
            cols = [
                {g: jnp.broadcast_to(rows[g][0][:, base + i : base + i + 1], (8, lanes)) for g in range(t, groups)}
                for i in range(8)
            ]
            for k in range(8):
                inv = lax.rsqrt(sub_row(cols[k][t], k))
                scaled = {g: cols[k][g] * inv for g in range(t, groups)}
                for j in range(k + 1, 8):
                    lj = sub_row(scaled[t], j)
                    for g in range(t, groups):
                        cols[j][g] = cols[j][g] - scaled[g] * lj
                below = jnp.where(sub > k, scaled[t], 0.0)
                for w in range(tiles):
                    rowk = sub_row(rows[t][w], k) * inv
                    rows[t][w] = jnp.where(sub == k, rowk, rows[t][w] - below * rowk)
                    for g in range(t + 1, groups):
                        rows[g][w] = rows[g][w] - scaled[g] * rowk
        done = jnp.concatenate([jnp.concatenate(rows[g], axis=1) for g in range(groups)], axis=0)
        work[r0 : r0 + sb, a0 : a0 + width] = done
        r1 = r0 + sb
        if r1 < n:
            b0 = r1 // lanes * lanes
            h, m, l = split3(done)
            left = jnp.concatenate([h, h, m, m, h, l], axis=0)[:, b0 - a0 : n - a0]
            right = jnp.concatenate([h, m, h, m, l, h], axis=0)
            update = lax.dot_general(left, right, (((0,), (0,)), ((), ())), preferred_element_type=F32)
            work[r1:n, a0 : a0 + width] = work[r1:n, a0 : a0 + width] - update[r1 - b0 :, :]


def per_device(R, C, tile_left, tile_right, tile_blocks, panel_left, panel_right, swap_flag):
    nb, rk = tile_left.shape[2:]
    blk, rp = panel_left.shape[2:]
    n = rk + rp
    NV = 4
    vm = pl.BlockSpec(memory_space=pltpu.VMEM)
    hbm = pl.BlockSpec(memory_space=pltpu.HBM)
    dma = pltpu.SemaphoreType.DMA
    S = jax.ShapeDtypeStruct
    V = pltpu.VMEM
    lo, ro = pl.pallas_call(
        functools.partial(update, R, C, NV),
        out_shape=(S((nb, n), BF16),) * 2,
        in_specs=[hbm] * 6,
        out_specs=[vm] * 2,
        scratch_shapes=[
            V((nb, rk), BF16), V((nb, rk), BF16), V((nb, rk), BF16), V((nb, rk), BF16), V((blk, rp), BF16),
            V((C, blk, rp), BF16), V((2, C, blk, rp), BF16), V((C, blk, rp), BF16),
            V((C, rp, rp), F32), V((C, rp, rp), BF16), V((C, rp, rp), BF16), V((8, 128), F32), V((C, 8, 128), F32),
            V((nb, n), BF16), V((n, 2 * n), F32), pltpu.SMEM((1, 1), jnp.int32), pltpu.SMEM((1, 1), jnp.int32),
            dma, dma, dma((NV,)), dma((NV,)), dma((C,)), dma((C,)), dma((C,)), dma((2, C, 3)), dma((2, C)), dma((2,)),
            dma((C, 3)), dma((C,)), dma((C,)), dma((C,)), dma((C,)), dma((C,)), dma((9,)),
        ],
        compiler_params=pltpu.CompilerParams(
            collective_id=0, has_side_effects=True, vmem_limit_bytes=58 * 1024 * 1024
        ),
        name="update",
    )(tile_left[0, 0], tile_right[0, 0], panel_left[:, 0], panel_right[:, 0], tile_blocks, swap_flag)
    return lo[None, None], ro[None, None]


def solution(mesh):
    placed = (
        P("row", "col", None, None),
        P("row", "col", None, None),
        P("row", "col"),
        P(None, "row", "col", None),
        P(None, "row", "col", None),
        P("row", "col"),
    )
    return jax.shard_map(
        functools.partial(per_device, mesh.shape["row"], mesh.shape["col"]),
        mesh=mesh,
        in_specs=placed,
        out_specs=(P("row", "col", None, None), P("row", "col", None, None)),
        check_vma=False,
    )
```

time: 70.1 us -> 46.6 us (0.66)
  the two profiles are of different devices: /device:TPU:29 before, /device:TPU:24 now
where the time goes in v1:
time: 46.6 us; the launch traced here: 46.4 us
  Pallas kernels  41.2 us (88%)
  local copies, waits for them, and re-layouts  3.32 us (7%)
  between operations  1.94 us (4%)
    pallas_call x1, Pallas kernels, per_device(): pl.pallas_call(functools.partial(update, R, C, NV), out_shape=(S((nb, n),...  41.2 us
    unnamed x4, local copies, waits for them, and re-layouts  3.32 us

profile of v1, /device:TPU:24, one launch (start us, length us, event | category | flops | bytes accessed | tf_op | source)
XLA Modules:
  0.0 46.4 jit_solution(12135239336011723016)
XLA Ops:
  1.9 41.2 %update.1 = (bf16[2048,256]{1,0:T(8,128)(2,1)}, bf16[2048,256]{1,0:T(8,128)(2,1)}) custom-call(bf16[2048,128]{1,0:T(8,128)(2,1)} %bitcast.8, bf16[2048,128]{1,0:T(8,128)(2,1)} %bitcast.9, bf16[2,512,128]{2,1,0:T(8,128)(2,1)} %bitcast.10, bf16[2,512,128]{2,1,0:T(8,128)(2,1)} %bitcast.11, s32[1,1]{1,0:T(1,128)S(6)} %copy.10.blocks, s32[1,1]{1,0:T(1,128)S(6)} %copy.11.swap), custom_call_target="tpu_custom_call" | custom-call | tf_op jit(solution)/shard_map/update/pallas_call | solution.py:331
  43.1 0.0 copy-start
  43.1 2.4 %copy.12 = bf16[1,1,2048,256]{3,2,1,0:T(8,128)(2,1)} copy(bf16[1,1,2048,256]{3,2,1,0:T(8,128)(2,1)} %bitcast.7) | data formatting | bytes 2097152
  45.4 0.0 copy-done
  45.4 1.0 %copy.13 = bf16[1,1,2048,256]{3,2,1,0:T(8,128)(2,1)} copy(bf16[1,1,2048,256]{3,2,1,0:T(8,128)(2,1)S(1)} %bitcast.6) | data formatting | bytes 2097152
Async XLA Ops:
  43.1 2.4 %copy-start = (bf16[2048,256]{1,0:T(8,128)(2,1)S(1)}, bf16[2048,256]{1,0:T(8,128)(2,1)}, u32[]{:S(2)}) copy-start(bf16[2048,256]{1,0:T(8,128)(2,1)} %get-tuple-element.5) | copy-start | bytes 3145732

commit v2 on v1

--- a/solution.py
+++ b/solution.py
@@ -13,9 +13,10 @@
 F32 = jnp.float32
 TN = (((0,), (0,)), ((), ()))
 NT = (((1,), (1,)), ((), ()))
-
-
-def update(R, C, NV, u, v, pleft, pright, blocks, swap, lo, ro,
+NN = (((1,), (0,)), ((), ()))
+
+
+def update(R, C, u, v, pleft, pright, blocks, swap, lo, ro,
            ubuf, vbuf, uown, vown, pr1, rowbuf, colbuf, prbuf, part, psend, precv, mine, mbuf, stack, work, sblk, sswp,
            s_u, r_u, s_v, r_v, s_row, r_row, s_fwd, s_col, r_col, s_st, s_pr, r_pr, s_part, r_part, s_meta, r_meta,
            s_loc):
@@ -29,6 +30,9 @@
     n = rk + rp
     tiles = (c, mate)
 
+    def nth(dev, k):
+        return lax.rem(dev + k, half) + half * lax.rem(dev // half + k // half, 2)
+
     def rcopy(src, dst, ss, rs, to):
         return pltpu.make_async_remote_copy(
             src_ref=src, dst_ref=dst, send_sem=ss, recv_sem=rs, device_id=to, device_id_type=MESH
@@ -90,21 +94,17 @@
     own_pr = (prbuf.at[at_r], s_pr.at[at_r], r_pr.at[at_r])
     for k, (cond, to) in enumerate(((has_up, r + 2), (has_dn, r - 2), (True, sib))):
         send((r < C) & cond, rcopy(pright.at[0], own_pr[0], own_pr[1].at[k], own_pr[2], (to, c)))
-    for d in range(C):
-        send((c != d) & (mate == d), rcopy(pleft.at[1], rowbuf.at[c], s_row.at[d], r_row.at[c], (r, d)))
-    for d in range(C):
-        same = (c // half) == d // half
-        send((c != d) & same & (mate != d), rcopy(pleft.at[1], rowbuf.at[c], s_row.at[d], r_row.at[c], (r, d)))
     for t in range(2):
         d = lax.rem(r + t * half, C)
         send((r < C) & (d != c), rcopy(pleft.at[0], colbuf.at[t, c], s_st.at[t], r_col.at[t, c], (r, d)))
 
-    for t in range(2):
-        slot, rs, ss = colbuf.at[t, c], r_col.at[t, c], s_col.at[t, c]
-        for k, (cond, to) in enumerate(((has_up, r + 2), (has_dn, r - 2), (True, sib))):
-            send((r == tiles[t]) & cond, rcopy(pleft.at[0], slot, ss.at[k], rs, (to, c)))
+    for d in range(C):
+        same = (c // half) == d // half
+        send((c != d) & same & (mate != d), rcopy(pleft.at[1], rowbuf.at[c], s_row.at[d], r_row.at[c], (r, d)))
     swap_u = rcopy(u, ubuf, s_u, r_u, (r, mate))
     swap_u.start()
+    for d in range(C):
+        send((c != d) & (mate == d), rcopy(pleft.at[1], rowbuf.at[c], s_row.at[d], r_row.at[c], (r, d)))
 
     load_r.wait()
 
@@ -135,7 +135,10 @@
                 send(r != s, rcopy(slot, slot, ss.at[2], rs, (sib, c)))
             part[s] = lax.dot_general(pr1[...], prbuf[s], TN, preferred_element_type=F32)
         if w == 0:
-            forward_row()
+            for t in range(2):
+                slot, rs, ss = colbuf.at[t, c], r_col.at[t, c], s_col.at[t, c]
+                for k, (cond, to) in enumerate(((has_up, r + 2), (has_dn, r - 2), (True, sib))):
+                    send((r == tiles[t]) & cond, rcopy(pleft.at[0], slot, ss.at[k], rs, (to, c)))
 
     for d in range(C):
         @pl.when(c != d)
@@ -155,44 +158,79 @@
     for d in range(C):
         send((c != d) & (mate != d), rcopy(psend.at[d], precv.at[c], s_part.at[d], r_part.at[c], (r, d)))
 
-    vb = nb // NV
-    swap_v = [rcopy(v.at[pl.ds(k * vb, vb)], vbuf.at[pl.ds(k * vb, vb)], s_v.at[k], r_v.at[k], (r, mate))
-              for k in range(NV)]
-    for copy in swap_v:
-        copy.start()
+    def v_chunk(b):
+        at = pl.ds(pl.multiple_of(b * blk, blk), blk)
+        return rcopy(v.at[at], vbuf.at[at], s_v.at[b], r_v.at[b], (r, mate))
+
+    for k in range(C):
+        v_chunk(nth(mate, k)).start()
 
     def away(t):
         return jnp.abs(r // 2 - tiles[t] // 2)
 
-    first = jnp.where(away(1) < away(0), 1, 0)
-    for t in (first, 1 - first):
+    near_t = jnp.where(away(1) < away(0), 1, 0)
+    far_t = 1 - near_t
+    far_home = jnp.where(far_t == 0, c, mate)
+    far_away = jnp.abs(r // 2 - far_home // 2)
+    early = far_away <= 1
+    ending = jnp.logical_not(early) & jnp.where(r > far_home, jnp.logical_not(has_up), jnp.logical_not(has_dn))
+
+    def pass_on(t, k, now):
         home = jnp.where(t == 0, c, mate)
-        par = lax.rem(r, 2) == lax.rem(home, 2)
-        for k in range(C):
-            b = lax.rem(c + k, half) + half * lax.rem(c // half + k // half, 2)
-            slot, rs, ss = colbuf.at[t, b], r_col.at[t, b], s_col.at[t, b]
-            relay = par & ((r != home) | (c != b))
-
-            @pl.when(relay)
-            def _():
-                rcopy(slot, slot, ss.at[0], rs, (sib, c)).wait_recv()
-
-            send(relay & (r >= home) & has_up, rcopy(slot, slot, ss.at[0], rs, (r + 2, c)))
-            send(relay & (r <= home) & has_dn, rcopy(slot, slot, ss.at[1], rs, (r - 2, c)))
-            send(relay, rcopy(slot, slot, ss.at[2], rs, (sib, c)))
+        b = nth(c, k)
+        slot, rs, ss = colbuf.at[t, b], r_col.at[t, b], s_col.at[t, b]
+        relay = (lax.rem(r, 2) == lax.rem(home, 2)) & ((r != home) | (c != b)) & now
+
+        @pl.when(relay)
+        def _():
+            rcopy(slot, slot, ss.at[0], rs, (sib, c)).wait_recv()
+
+        send(relay & (r >= home) & has_up, rcopy(slot, slot, ss.at[0], rs, (r + 2, c)))
+        send(relay & (r <= home) & has_dn, rcopy(slot, slot, ss.at[1], rs, (r - 2, c)))
+        send(relay, rcopy(slot, slot, ss.at[2], rs, (sib, c)))
+
+    for k in range(C):
+        pass_on(near_t, k, True)
+    for k in range(C):
+        pass_on(far_t, k, early)
+    inside = jnp.logical_not(early | ending)
 
     chosen_meta = jnp.where(flagged, mbuf[mate], own_meta)
     lane = lax.broadcasted_iota(jnp.int32, (1, rk), 1).astype(F32)
     live = lane < chosen_meta[1:2, :] * RBLK
     zero = jnp.zeros((), BF16)
 
-    load_l.wait()
-    for d in range(C):
-        @pl.when((c != d) & (mate != d))
-        def _():
-            rcopy(pleft.at[1], rowbuf.at[d], s_row.at[d], r_row.at[d], (r, d)).wait_recv()
+    def sliced(step):
+        return pl.ds(pl.multiple_of(step * blk, blk), blk)
+
     load_u.wait()
     swap_u.wait_recv()
+
+    def fill(step, acc):
+        left = jnp.where(live, jnp.where(flagged, ubuf[sliced(step), :], uown[sliced(step), :]), zero)
+        stack[sliced(step), :rk] = left
+        return acc + lax.dot_general(left, left, TN, preferred_element_type=F32)
+
+    g11 = lax.fori_loop(0, C, fill, jnp.zeros((rk, rk), F32), unroll=True) / nb
+    dead = jnp.where(live, 0.0, 1.0).astype(F32)
+    eye = jnp.where(
+        lax.broadcasted_iota(jnp.int32, (rk, rk), 0) == lax.broadcasted_iota(jnp.int32, (rk, rk), 1), 1.0, 0.0
+    ).astype(F32)
+    work[:, :rk] = g11 + eye * dead
+    work[:, rk:] = eye
+    factor_rows(work, rk, 64)
+    forward_row()
+    pass_on(far_t, 0, inside)
+    upper = jnp.where(
+        lax.broadcasted_iota(jnp.int32, (rk, rk), 0) <= lax.broadcasted_iota(jnp.int32, (rk, rk), 1), 1.0, 0.0
+    ).astype(F32)
+    u11, i11 = work[:, :rk] * upper, work[:, rk:]
+
+    load_l.wait()
+    for d in range(C):
+        @pl.when((c != d) & (mate != d))
+        def _():
+            rcopy(pleft.at[1], rowbuf.at[d], s_row.at[d], r_row.at[d], (r, d)).wait_recv()
     for d in range(C):
         @pl.when(c != d)
         def _():
@@ -205,59 +243,70 @@
         total = total + precv[d].astype(F32)
     coup = total.astype(BF16)
 
-    def fill(step, acc):
-        at = pl.ds(pl.multiple_of(step * blk, blk), blk)
-        lifted = -jnp.dot(rowbuf[step], coup, preferred_element_type=F32)
-        left = jnp.where(flagged, ubuf[at, :], uown[at, :])
-        piece = jnp.concatenate([jnp.where(live, left, zero), lifted.astype(BF16)], axis=1)
-        stack[at, :] = piece
-        return acc + lax.dot_general(piece, piece, TN, preferred_element_type=F32)
-
-    gram = lax.fori_loop(0, C, fill, jnp.zeros((n, n), F32)) / nb
-    ri = lax.broadcasted_iota(jnp.int32, (n, n), 0)
-    ci = lax.broadcasted_iota(jnp.int32, (n, n), 1)
-    dead = jnp.concatenate([jnp.where(live, 0.0, 1.0).astype(F32), jnp.zeros((1, rp), F32)], axis=1)
-    work[:, :n] = gram + jnp.where(ri == ci, dead, 0.0)
-    work[:, n:] = jnp.where(ri == ci, 1.0, 0.0).astype(F32)
-    factor_rows(work, n, 32)
-    uph, upm, _ = split3(jnp.where(ri <= ci, work[:, :n], 0.0))
-    inh, inm, _ = split3(work[:, n:])
+    def lift(step, acc):
+        lifted = (-jnp.dot(rowbuf[step], coup, preferred_element_type=F32)).astype(BF16)
+        stack[sliced(step), rk:] = lifted
+        return acc + lax.dot_general(stack[sliced(step), :], lifted, TN, preferred_element_type=F32)
+
+    g2 = lax.fori_loop(0, C, lift, jnp.zeros((n, rp), F32), unroll=True) / nb
+    pass_on(far_t, 1, inside)
+
+    def exact(x, y, dims):
+        return lax.dot_general(x, y, dims, precision=lax.Precision.HIGHEST, preferred_element_type=F32)
+
+    u12 = exact(i11, g2[:rk, :], NN)
+    work[:, :rp] = g2[rk:, :] - exact(u12, u12, TN)
+    work[:, rp:] = eye
+    factor_rows(work, rp, 64)
+    pass_on(far_t, 2, inside)
+    u22, i22 = work[:, :rp] * upper, work[:, rp:]
+    i21 = -exact(i22, exact(u12, i11, TN), NN)
+    none = jnp.zeros((rk, rp), F32)
+    uph, upm, _ = split3(jnp.concatenate(
+        [jnp.concatenate([u11, u12], axis=1), jnp.concatenate([none, u22], axis=1)], axis=0))
+    inh, inm, _ = split3(jnp.concatenate(
+        [jnp.concatenate([i11, none], axis=1), jnp.concatenate([i21, i22], axis=1)], axis=0))
+    pass_on(far_t, 3, inside)
+    for k in range(4, C):
+        pass_on(far_t, k, inside)
 
     def product(value, high, low):
         out = lax.dot_general(value, high, NT, preferred_element_type=F32)
         return (out + lax.dot_general(value, low, NT, preferred_element_type=F32)).astype(BF16)
 
-    def left_step(step, _):
-        at = pl.ds(pl.multiple_of(step * vb, vb), vb)
-        lo[at, :] = product(stack[at, :], inh, inm)
-        return 0
-
-    lax.fori_loop(0, NV, left_step, 0)
+    lo[...] = product(stack[...], inh, inm)
+    for k in range(C):
+        pass_on(far_t, k, ending)
 
     load_v.wait()
     for t in range(2):
         @pl.when(r == tiles[t])
         def _():
             load_c[t].wait()
-
-        for b in range(C):
+    def arrived(k):
+        b = nth(c, k)
+        for t in range(2):
             @pl.when(lax.rem(r, 2) != lax.rem(tiles[t], 2))
             def _():
                 rcopy(colbuf.at[t, b], colbuf.at[t, b], s_col.at[t, b, 0], r_col.at[t, b], (sib, c)).wait_recv()
-
-    for k in range(NV):
-        swap_v[k].wait_recv()
-        at = pl.ds(k * vb, vb)
-        right = jnp.where(live, jnp.where(flagged, vbuf[at, :], vown[at, :]), zero)
-        first, count = k * vb // blk, max(vb // blk, 1)
-        cols = pl.ds(k * vb % blk, min(vb, blk))
-        own = [jnp.where(flagged, colbuf[1, first + i, cols, :], colbuf[0, first + i, cols, :]) for i in range(count)]
-        pair = jnp.concatenate([right, jnp.concatenate(own, axis=0)], axis=1)
-        ro[at, :] = product(pair, uph, upm)
-
+        v_chunk(b).wait_recv()
+
+    def right_rows(k):
+        b = nth(c, k)
+        right = jnp.where(live, jnp.where(flagged, vbuf[sliced(b), :], vown[sliced(b), :]), zero)
+        own = jnp.where(flagged, colbuf[1, b], colbuf[0, b])
+        return jnp.concatenate([right, own], axis=1)
+
+    for group in (range(C - 1), range(C - 1, C)):
+        for k in group:
+            arrived(k)
+        out = product(jnp.concatenate([right_rows(k) for k in group], axis=0), uph, upm)
+        for i, k in enumerate(group):
+            ro[sliced(nth(c, k)), :] = out[i * blk : (i + 1) * blk, :]
+
+    for b in range(C):
+        v_chunk(b).wait_send()
     swap_u.wait_send()
-    for copy in swap_v:
-        copy.wait_send()
     for cond, copy in ends:
         @pl.when(cond)
         def _():
@@ -322,23 +371,21 @@
     nb, rk = tile_left.shape[2:]
     blk, rp = panel_left.shape[2:]
     n = rk + rp
-    NV = 4
     vm = pl.BlockSpec(memory_space=pltpu.VMEM)
     hbm = pl.BlockSpec(memory_space=pltpu.HBM)
     dma = pltpu.SemaphoreType.DMA
-    S = jax.ShapeDtypeStruct
     V = pltpu.VMEM
     lo, ro = pl.pallas_call(
-        functools.partial(update, R, C, NV),
-        out_shape=(S((nb, n), BF16),) * 2,
+        functools.partial(update, R, C),
+        out_shape=(pltpu.VMEM((nb, n), BF16),) * 2,
         in_specs=[hbm] * 6,
         out_specs=[vm] * 2,
         scratch_shapes=[
             V((nb, rk), BF16), V((nb, rk), BF16), V((nb, rk), BF16), V((nb, rk), BF16), V((blk, rp), BF16),
             V((C, blk, rp), BF16), V((2, C, blk, rp), BF16), V((C, blk, rp), BF16),
             V((C, rp, rp), F32), V((C, rp, rp), BF16), V((C, rp, rp), BF16), V((8, 128), F32), V((C, 8, 128), F32),
-            V((nb, n), BF16), V((n, 2 * n), F32), pltpu.SMEM((1, 1), jnp.int32), pltpu.SMEM((1, 1), jnp.int32),
-            dma, dma, dma((NV,)), dma((NV,)), dma((C,)), dma((C,)), dma((C,)), dma((2, C, 3)), dma((2, C)), dma((2,)),
+            V((nb, n), BF16), V((rk, 2 * rk), F32), pltpu.SMEM((1, 1), jnp.int32), pltpu.SMEM((1, 1), jnp.int32),
+            dma, dma, dma((C,)), dma((C,)), dma((C,)), dma((C,)), dma((C,)), dma((2, C, 3)), dma((2, C)), dma((2,)),
             dma((C, 3)), dma((C,)), dma((C,)), dma((C,)), dma((C,)), dma((C,)), dma((9,)),
         ],
         compiler_params=pltpu.CompilerParams(

time: 46.6 us -> 42.7 us (0.916); the launches traced: 46.4 us -> 42 us
  Pallas kernels: 41.2 us -> 38.1 us
  local copies, waits for them, and re-layouts: 3.32 us -> 1.94 us
    pallas_call x1, Pallas kernels: 41.2 us -> 38.1 us  [per_device(): pl.pallas_call(functools.partial(update, R, C), out_shape=(pltpu.VMEM((nb...]
    unnamed x4 -> x2, local copies, waits for them, and re-layouts: 3.32 us -> 1.94 us
where the time goes in v2:
time: 42.7 us; the launch traced here: 42 us
  Pallas kernels  38.1 us (89%)
  local copies, waits for them, and re-layouts  1.94 us (5%)
  between operations  1.93 us (5%)
    pallas_call x1, Pallas kernels, per_device(): pl.pallas_call(functools.partial(update, R, C), out_shape=(pltpu.VMEM((nb...  38.1 us
    unnamed x2, local copies, waits for them, and re-layouts  1.94 us

profile of v2, /device:TPU:24, one launch (start us, length us, event | category | flops | bytes accessed | tf_op | source)
XLA Modules:
  0.0 42.0 jit_solution(11597321468031172542)
XLA Ops:
  1.9 38.1 %update.1 = (bf16[2048,256]{1,0:T(8,128)(2,1)S(1)}, bf16[2048,256]{1,0:T(8,128)(2,1)S(1)}) custom-call(bf16[2048,128]{1,0:T(8,128)(2,1)} %bitcast.8, bf16[2048,128]{1,0:T(8,128)(2,1)} %bitcast.9, bf16[2,512,128]{2,1,0:T(8,128)(2,1)} %bitcast.10, bf16[2,512,128]{2,1,0:T(8,128)(2,1)} %bitcast.11, s32[1,1]{1,0:T(1,128)S(6)} %copy.12.blocks, s32[1,1]{1,0:T(1,128)S(6)} %copy.13.swap), custom_call_target="tpu_custom_call" | custom-call | tf_op jit(solution)/shard_map/update/pallas_call | solution.py:378
  40.0 1.0 %copy.10 = bf16[1,1,2048,256]{3,2,1,0:T(8,128)(2,1)} copy(bf16[1,1,2048,256]{3,2,1,0:T(8,128)(2,1)S(1)} %bitcast.7) | data formatting | bytes 2097152
  41.0 1.0 %copy.11 = bf16[1,1,2048,256]{3,2,1,0:T(8,128)(2,1)} copy(bf16[1,1,2048,256]{3,2,1,0:T(8,128)(2,1)S(1)} %bitcast.6) | data formatting | bytes 2097152
